TPU v7x, 32 devices: a whole 2x2x4 slice. The times are simulated.
32 devices in a mesh: dp: 2 (over x), expert: 16 (over z, y, core).
Axes of the slice: x: 2, y: 2, z: 4, core: 2. Of those that a mesh axis runs over, the one named last changes fastest.
Arguments:
- tokens: bfloat16 [4096, 2048], P(('dp', 'expert')), may hold values from -160 to 160
- router_weight: bfloat16 [2048, 16], replicated, may hold values from -0.25 to 0.25
- route_ids: int32 [4096, 2], P(('dp', 'expert')), may hold values from 0 to 15, as said below
- gate_weight: bfloat16 [16, 768, 2048], P('expert', 'dp'), may hold values from -0.125 to 0.125
- up_weight: bfloat16 [16, 768, 2048], P('expert', 'dp'), may hold values from -0.125 to 0.125
- down_weight: bfloat16 [16, 768, 2048], P('expert', 'dp'), may hold values from -0.21875 to 0.21875
Outputs:
- mixture: bfloat16 [4096, 2048], P(('dp', 'expert'))
- z_loss: float32 [], replicated
Inputs may be any that keep to these rules, and one draw needn't show every extreme that they name: `route_ids`: each row names 2 different experts; among the rows of one device no expert is named more than 20 times, and one expert is named exactly 20 times by the rows of every device.
All inputs are finite; a program needn't handle non-finite values.
Results may differ from a plain program's by a relative error of at most 0.0057.
Values may be sent and summed in bfloat16 or wider, within the bound.
No kernel may reach another device: no remote copies, remote signals or barrier semaphores. Data moves between devices by JAX's collectives and lax.ppermute only.
A program may use at most 64 MiB of HBM per device.

v0:
```python
import jax
import jax.numpy as jnp
from jax import lax
from jax.sharding import PartitionSpec as P


def slot_index(route_ids, experts, capacity):
    flat_ids = route_ids.reshape(-1)
    onehot = (flat_ids[:, None] == jnp.arange(experts, dtype=jnp.int32)[None, :]).astype(jnp.int32)
    before = jnp.cumsum(onehot, axis=0) - onehot
    position = jnp.sum(before * onehot, axis=1)
    return flat_ids * capacity + position


def on_device(tokens, router_weight, route_ids, gate_weight, up_weight, down_weight):
    rows_here, model_width = tokens.shape
    top_count = route_ids.shape[1]
    experts = router_weight.shape[1]
    owners = lax.axis_size("expert")
    local_experts = gate_weight.shape[0]
    capacity = 5 * rows_here * top_count // (4 * experts)
    logits = jnp.dot(tokens, router_weight, preferred_element_type=jnp.float32)
    log_total = jax.nn.logsumexp(logits, axis=1)
    local_sum = jnp.sum(log_total * log_total)
    chosen = jnp.take_along_axis(logits, route_ids, axis=1)
    route_weight = jax.nn.softmax(chosen, axis=1)
    slots = slot_index(route_ids, experts, capacity)
    pair_count = slots.shape[0]
    slot_match = slots[None, :] == jnp.arange(experts * capacity, dtype=jnp.int32)[:, None]
    token_of = jnp.arange(pair_count, dtype=jnp.int32) // top_count
    source_row = jnp.sum(jnp.where(slot_match, token_of[None, :], 0), axis=1)
    filled = jnp.any(slot_match, axis=1)
    dispatch = jnp.where(filled[:, None], tokens[source_row], jnp.zeros((), tokens.dtype))
    dispatch = dispatch.reshape(experts, capacity, model_width)
    received = lax.all_to_all(dispatch, "expert", split_axis=0, concat_axis=0, tiled=True)
    expert_rows = received.reshape(owners, local_experts, capacity, model_width)
    expert_rows = expert_rows.transpose(1, 0, 2, 3).reshape(
        local_experts, owners * capacity, model_width
    )
    gate_piece, up_piece = lax.all_gather((gate_weight, up_weight), "dp", axis=1, tiled=True)
    gate_val = jnp.einsum(
        "erd,efd->erf", expert_rows, gate_piece, preferred_element_type=jnp.float32
    )
    up_val = jnp.einsum("erd,efd->erf", expert_rows, up_piece, preferred_element_type=jnp.float32)
    hidden_all = (jax.nn.silu(gate_val) * up_val).astype(jnp.bfloat16)
    summed = jnp.einsum(
        "erf,efd->erd",
        hidden_all,
        lax.all_gather(down_weight, "dp", axis=1, tiled=True),
        preferred_element_type=jnp.float32,
    )
    expert_out = summed.astype(jnp.bfloat16)
    outgoing = expert_out.reshape(local_experts, owners, capacity, model_width)
    outgoing = outgoing.transpose(1, 0, 2, 3).reshape(experts, capacity, model_width)
    returned = lax.all_to_all(outgoing, "expert", split_axis=0, concat_axis=0, tiled=True)
    flat_rows = returned.reshape(experts * capacity, model_width)
    picked = flat_rows[slots].reshape(rows_here, top_count, model_width)
    mixed_out = jnp.sum(route_weight[:, :, None] * picked.astype(jnp.float32), axis=1).astype(
        jnp.bfloat16
    )
    total_sum = lax.psum(local_sum, ("dp", "expert"))
    token_total = rows_here * lax.axis_size("dp") * owners
    z_loss = total_sum / jnp.float32(token_total)
    return (mixed_out, z_loss)


def solution(mesh):
    in_specs = (
        P(("dp", "expert"), None),
        P(),
        P(("dp", "expert"), None),
        P("expert", "dp", None),
        P("expert", "dp", None),
        P("expert", "dp", None),
    )
    out_specs = (P(("dp", "expert"), None), P())
    return jax.shard_map(
        on_device, mesh=mesh, in_specs=in_specs, out_specs=out_specs, check_vma=False
    )
```

profile of v0, /device:TPU:0, one launch (start us, length us, event | category | flops | bytes accessed | tf_op | source)
XLA Modules:
  0.0 240.4 jit_solution(12554654109535446574)
XLA Ops:
  7.2 0.7 all-gather.4.cloned.1.call-update
  8.0 0.7 all-gather.6.cloned.1.call-update
  8.7 0.7 all-gather.8.cloned.1.call-update
  9.8 0.6 reduce-window.6
  10.4 0.2 slice_reduce_fusion
  11.1 2.4 %gather_fusion = bf16[320,2048]{1,0:T(8,128)(2,1)S(1)} fusion(bf16[128,2048]{1,0:T(8,128)(2,1)S(1)} %copy-done, s32[1024]{0:T(1024)S(1)} %pad_clamp_fusion.1), kind=kCustom, calls=%fused_computation | custom fusion | bytes 2622720 | tf_op jit(solution)/shard_map/gather | solution.py:33
  13.5 0.3 gather.14
  14.0 0.2 broadcast_select_fusion
  14.2 43.1 %all_to_all.10 = bf16[16,20,2048]{2,1,0:T(8,128)(2,1)S(1)} all-to-all(bf16[16,20,2048]{2,1,0:T(8,128)(2,1)S(1)} %broadcast_select_fusion), channel_id=1, replica_groups=mesh['dp'=2,'expert'=16] {'expert'}, dimensions={0} | all-to-all | bytes 2621440 | tf_op jit(solution)/shard_map/all_to_all | solution.py:35
  57.3 0.3 reshape.165
  57.6 4.1 %fusion.4 = f32[320,768]{1,0:T(8,128)} fusion(bf16[320,2048]{1,0:T(8,128)(2,1)S(1)} %reshape.165, bf16[1,768,2048]{2,1,0:T(8,128)(2,1)} %all-gather.4.cloned.1.call-done), kind=kOutput, calls=%fused_computation.7 | convolution fusion | flops 1006632960 | bytes 5439488 | tf_op jit(solution)/shard_map/erd,efd->erf/dot_general | solution.py:41
  61.7 42.0 %all-gather.6.cloned.1.call-done = bf16[1,768,2048]{2,1,0:T(8,128)(2,1)} async-done(((bf16[1,384,2048]{2,1,0:T(8,128)(2,1)}), bf16[1,768,2048]{2,1,0:T(8,128)(2,1)}) %all-gather.6.cloned.1.call-update) | async-done | bytes 3145744 | tf_op jit(solution)/shard_map/all_gather | solution.py:40
  103.7 46.5 %all-gather.8.cloned.1.call-done = bf16[1,768,2048]{2,1,0:T(8,128)(2,1)} async-done(((bf16[1,384,2048]{2,1,0:T(8,128)(2,1)}), bf16[1,768,2048]{2,1,0:T(8,128)(2,1)}) %all-gather.8.cloned.1.call-update) | async-done | bytes 3145744 | tf_op jit(solution)/shard_map/all_gather | solution.py:49
  150.2 5.8 %fusion.6 = bf16[320,2048]{1,0:T(8,128)(2,1)S(1)} fusion(bf16[1,768,2048]{2,1,0:T(8,128)(2,1)} %all-gather.8.cloned.1.call-done, bf16[320,2048]{1,0:T(8,128)(2,1)S(1)} %reshape.165, bf16[1,768,2048]{2,1,0:T(8,128)(2,1)} %all-gather.6.cloned.1.call-done, f32[320,768]{1,0:T(8,128)} %fusion.4), kind=kOutput, calls=%fused_computation.9 | convolution fusion | flops 2015395840 | bytes 9895936 | tf_op jit(solution)/shard_map/erf,efd->erd/dot_general | solution.py:46
  155.9 1.3 reshape_transpose_reshape.4
  157.3 5.8 %all-to-all-start.1 = ((bf16[16,20,2048]{2,1,0:T(8,128)(2,1)}), bf16[16,20,2048]{2,1,0:T(8,128)(2,1)S(1)}, u32[]{:S(2)}, u32[]{:S(2)}) async-start(bf16[16,20,2048]{2,1,0:T(8,128)(2,1)} %reshape_transpose_reshape.4), calls=%async_computation.1 | async-start | bytes 3145728 | tf_op jit(solution)/shard_map/all_to_all | solution.py:55
  163.0 0.3 fusion.28
  163.3 0.6 multiply_reduce_fusion.1
  163.9 56.2 %psum.7 = f32[]{:T(128)} all-reduce(f32[]{:T(128)} %multiply_reduce_fusion.1), channel_id=1, replica_groups=mesh['dp'=2,'expert'=16] {'dp','expert'}, use_global_device_ids=true, to_apply=%region_11.12 | all-reduce | flops 1 | bytes 8 | tf_op jit(solution)/shard_map/psum | solution.py:61
  220.6 2.0 gather_fusion.2
  223.7 0.3 reshape.169
  224.0 2.3 gather_fusion.1
  226.4 2.4 reshape.170
  228.8 3.9 %multiply_reduce_fusion = bf16[128,2048]{1,0:T(8,128)(2,1)} fusion(f32[128,2,2048]{2,1,0:T(2,128)S(1)} %reshape.170, f32[128,2]{1,0:T(8,128)S(1)} %copy.29), kind=kLoop, calls=%fused_computation.10 | loop fusion | flops 786432 | bytes 2622464 | tf_op jit(solution)/shard_map/reduce_sum | solution.py:58
  (40 shorter events, 2.1 us)
Async XLA Ops:
  7.2 3.9 %copy-start = (bf16[128,2048]{1,0:T(8,128)(2,1)S(1)}, bf16[128,2048]{1,0:T(8,128)(2,1)}, u32[]{:S(2)}) copy-start(bf16[128,2048]{1,0:T(8,128)(2,1)} %param.6) | copy-start | bytes 1572868
  7.2 50.4 %all-gather.4.cloned.1.call-start = ((), (), s32[]{:S(2)}) async-start(), calls=%async_computation.2 | async-start | bytes 4718592 | tf_op jit(solution)/shard_map/all_gather | solution.py:40
  7.9 1.5 copy-start.2
  7.9 95.8 %all-gather.6.cloned.1.call-start = ((), (), s32[]{:S(2)}) async-start(), calls=%async_computation.3 | async-start | bytes 4718592 | tf_op jit(solution)/shard_map/all_gather | solution.py:40
  8.7 141.5 %all-gather.8.cloned.1.call-start = ((), (), s32[]{:S(2)}) async-start(), calls=%async_computation.4 | async-start | bytes 4718592 | tf_op jit(solution)/shard_map/all_gather | solution.py:49
  157.3 5.8 %copy-start.1 = (bf16[2048,16]{0,1:T(8,128)(2,1)S(1)}, bf16[2048,16]{0,1:T(8,128)(2,1)}, u32[]{:S(2)}) copy-start(bf16[2048,16]{0,1:T(8,128)(2,1)} %param.7) | copy-start | bytes 196612
  157.3 66.5 %all-to-all-start.1 = ((bf16[16,20,2048]{2,1,0:T(8,128)(2,1)}), bf16[16,20,2048]{2,1,0:T(8,128)(2,1)S(1)}, u32[]{:S(2)}, u32[]{:S(2)}) async-start(bf16[16,20,2048]{2,1,0:T(8,128)(2,1)} %reshape_transpose_reshape.4), calls=%async_computation.1 | async-start | bytes 3145728 | tf_op jit(solution)/shard_map/all_to_all | solution.py:55
Sparse Core Ops, SparseCore 0:
  9.5 47.6 all-gather.3
  58.7 44.8 all-gather.5
  105.2 44.8 all-gather.7
where the time goes:
time: 241 us; the launch traced here: 240 us
  blocking collectives  99.3 us (41%)
  waiting for transfers between devices  90.6 us (38%)
  between operations  15.8 us (7%)
  local copies, waits for them, and re-layouts  12.9 us (5%)
  matrix products  10.1 us (4%)
  other arithmetic  5.91 us (2%)
  starting transfers between devices  5.87 us (2%)
    psum x1, blocking collectives, on_device(): total_sum = lax.psum(local_sum, ('dp', 'expert'))  56.2 us
    all_gather x1, waiting for transfers between devices, on_device(): lax.all_gather(down_weight, 'dp', axis=1, tiled=True)  46.5 us
    all_to_all x1, blocking collectives, on_device(): lax.all_to_all(dispatch, 'expert', split_axis=0, concat_axis=0, tiled=True)  43.1 us
    all_gather x2, waiting for transfers between devices, on_device(): lax.all_gather((gate_weight, up_weight), 'dp', axis=1, tiled=True)  42 us
    dot_general x1, matrix products, on_device(): jnp.einsum('erf,efd->erd', hidden_all, lax.all_gather(down_weight, 'dp',...  5.77 us
    all_to_all x1, starting transfers between devices, on_device(): lax.all_to_all(outgoing, 'expert', split_axis=0, concat_axis=0, tiled=True)  5.75 us
  transfers between devices with their start and end apart: 4, of which 2 were waited for; matrix products, arithmetic and copies ran while one was open for 5% of the time, Pallas kernels for 0%

commit v1 on v0

--- a/solution.py
+++ b/solution.py
@@ -2,6 +2,22 @@
 import jax.numpy as jnp
 from jax import lax
 from jax.sharding import PartitionSpec as P
+
+
+def refer_sectors(local_block, tile_in):
+    new = lax.psum(1, "dp")
+    a_next = lax.axis_index("dp")
+    earlier, odd, r1 = (new, a_next, local_block.shape[1])
+    w_next, known = (local_block, None)
+    windows = [(t, (t + 1) % earlier) for t in range(earlier)]
+    j0 = 0
+    while j0 < earlier:
+        found_now = lax.ppermute(w_next, "dp", perm=windows) if j0 < earlier - 1 else None
+        formed = tile_in(w_next, (odd - j0) % earlier * r1)
+        known = formed if known is None else known + formed
+        w_next = found_now
+        j0 = j0 + 1
+    return known
 
 
 def slot_index(route_ids, experts, capacity):
@@ -43,11 +59,14 @@
     )
     up_val = jnp.einsum("erd,efd->erf", expert_rows, up_piece, preferred_element_type=jnp.float32)
     hidden_all = (jax.nn.silu(gate_val) * up_val).astype(jnp.bfloat16)
-    summed = jnp.einsum(
-        "erf,efd->erd",
-        hidden_all,
-        lax.all_gather(down_weight, "dp", axis=1, tiled=True),
-        preferred_element_type=jnp.float32,
+    summed = refer_sectors(
+        down_weight,
+        lambda own_block, offset: jnp.einsum(
+            "erf,efd->erd",
+            lax.dynamic_slice_in_dim(hidden_all, offset, own_block.shape[1], axis=2),
+            own_block,
+            preferred_element_type=jnp.float32,
+        ),
     )
     expert_out = summed.astype(jnp.bfloat16)
     outgoing = expert_out.reshape(local_experts, owners, capacity, model_width)

time: 241 us -> 227 us (0.942)
  blocking collectives: 99.3 us -> 56.2 us
  waiting for transfers between devices: 90.6 us -> 109 us
  starting transfers between devices: 5.87 us -> 14.8 us
    all_gather x1 -> x0, waiting for transfers between devices: 46.5 us -> none  [on_device(): lax.all_gather(down_weight, 'dp', axis=1, tiled=True)]
    all_to_all x1 -> x0, blocking collectives: 43.1 us -> none  [on_device(): lax.all_to_all(dispatch, 'expert', split_axis=0, concat_axis=0, tiled=True)]
    all_gather x2, waiting for transfers between devices: 42 us -> 76.8 us  [on_device(): lax.all_gather((gate_weight, up_weight), 'dp', axis=1, tiled=True)]
    all_to_all x0 -> x1, waiting for transfers between devices: none -> 30.3 us  [on_device(): lax.all_to_all(dispatch, 'expert', split_axis=0, concat_axis=0, tiled=True)]
    all_to_all x0 -> x1, starting transfers between devices: none -> 7.41 us  [on_device(): lax.all_to_all(dispatch, 'expert', split_axis=0, concat_axis=0, tiled=True)]
    dot_general x1 -> x3, matrix products: 5.77 us -> 6.53 us  [the longest x1 3.39 us: on_device(): jnp.einsum('erd,efd->erf', expert_rows, up_piece, preferred_element_type=...]
  transfers between devices with their start and end apart: 4 -> 5, of which waited for: 2 -> 3; matrix products, arithmetic and copies ran while one was open for 5% -> 8% of each run, Pallas kernels for 0% -> 0%
where the time goes in v1:
time: 227 us
  waiting for transfers between devices  109 us (48%)
  blocking collectives  56.2 us (25%)
  between operations  16.1 us (7%)
  starting transfers between devices  14.8 us (7%)
  local copies, waits for them, and re-layouts  12.9 us (6%)
  matrix products  10.9 us (5%)
  other arithmetic  7.15 us (3%)
    all_gather x2, waiting for transfers between devices, on_device(): lax.all_gather((gate_weight, up_weight), 'dp', axis=1, tiled=True)  76.8 us
    psum x1, blocking collectives, on_device(): total_sum = lax.psum(local_sum, ('dp', 'expert'))  56.2 us
    all_to_all x1, waiting for transfers between devices, on_device(): lax.all_to_all(dispatch, 'expert', split_axis=0, concat_axis=0, tiled=True)  30.3 us
    all_to_all x1, starting transfers between devices, on_device(): lax.all_to_all(dispatch, 'expert', split_axis=0, concat_axis=0, tiled=True)  7.41 us
    all_to_all x1, starting transfers between devices, on_device(): lax.all_to_all(outgoing, 'expert', split_axis=0, concat_axis=0, tiled=True)  5.75 us
  transfers between devices with their start and end apart: 5, of which 3 were waited for; matrix products, arithmetic and copies ran while one was open for 8% of the time, Pallas kernels for 0%

profile of v1, /device:TPU:0, one launch (start us, length us, event | category | flops | bytes accessed | tf_op | source)
XLA Modules:
  0.0 226.5 jit_solution(14715360825186800267)
XLA Ops:
  7.2 0.7 all-gather.3.cloned.1.call-update
  8.0 0.7 all-gather.5.cloned.1.call-update
  9.1 0.6 reduce-window.6
  10.4 2.4 %gather_fusion = bf16[320,2048]{1,0:T(8,128)(2,1)S(1)} fusion(bf16[128,2048]{1,0:T(8,128)(2,1)S(1)} %copy-done, s32[1024]{0:T(1024)S(1)} %pad_clamp_fusion.1), kind=kCustom, calls=%fused_computation | custom fusion | bytes 2622720 | tf_op jit(solution)/shard_map/gather | solution.py:49
  12.8 0.3 gather.14
  13.2 1.4 broadcast_select_fusion
  14.6 7.4 %all-to-all-start = ((bf16[16,20,2048]{2,1,0:T(8,128)(2,1)}), bf16[16,20,2048]{2,1,0:T(8,128)(2,1)S(1)}, u32[]{:S(2)}, u32[]{:S(2)}) async-start(bf16[16,20,2048]{2,1,0:T(8,128)(2,1)} %broadcast_select_fusion), calls=%async_computation | async-start | bytes 3145728 | tf_op jit(solution)/shard_map/all_to_all | solution.py:51
  22.1 1.6 collective-permute-start
  23.6 30.3 %all-to-all-done = bf16[16,20,2048]{2,1,0:T(8,128)(2,1)S(1)} async-done(((bf16[16,20,2048]{2,1,0:T(8,128)(2,1)}), bf16[16,20,2048]{2,1,0:T(8,128)(2,1)S(1)}, u32[]{:S(2)}, u32[]{:S(2)}) %all-to-all-start) | async-done | bytes 1310752 | tf_op jit(solution)/shard_map/all_to_all | solution.py:51
  54.2 34.7 %all-gather.3.cloned.1.call-done = bf16[1,768,2048]{2,1,0:T(8,128)(2,1)} async-done(((bf16[1,384,2048]{2,1,0:T(8,128)(2,1)}), bf16[1,768,2048]{2,1,0:T(8,128)(2,1)}) %all-gather.3.cloned.1.call-update) | async-done | bytes 3145744 | tf_op jit(solution)/shard_map/all_gather | solution.py:56
  88.9 4.2 %fusion.2 = f32[320,768]{1,0:T(8,128)} fusion(bf16[320,2048]{1,0:T(8,128)(2,1)S(1)} %reshape.174, bf16[1,768,2048]{2,1,0:T(8,128)(2,1)} %all-gather.3.cloned.1.call-done), kind=kOutput, calls=%fused_computation.5 | convolution fusion | flops 1006632960 | bytes 5439488 | tf_op jit(solution)/shard_map/erd,efd->erf/dot_general | solution.py:57
  93.1 42.1 %all-gather.5.cloned.1.call-done = bf16[1,768,2048]{2,1,0:T(8,128)(2,1)} async-done(((bf16[1,384,2048]{2,1,0:T(8,128)(2,1)}), bf16[1,768,2048]{2,1,0:T(8,128)(2,1)}) %all-gather.5.cloned.1.call-update) | async-done | bytes 3145744 | tf_op jit(solution)/shard_map/all_gather | solution.py:56
  135.2 3.4 %fusion.11 = bf16[320,768]{1,0:T(8,128)(2,1)S(1)} fusion(bf16[320,2048]{1,0:T(8,128)(2,1)S(1)} %reshape.174, bf16[1,768,2048]{2,1,0:T(8,128)(2,1)} %all-gather.5.cloned.1.call-done, f32[320,768]{1,0:T(8,128)} %fusion.2), kind=kOutput, calls=%fused_computation.15 | convolution fusion | flops 1008107520 | bytes 5931008 | tf_op jit(solution)/shard_map/erd,efd->erf/dot_general | solution.py:60
  138.6 0.8 fusion.6
  139.5 2.3 %fusion.4 = bf16[320,2048]{1,0:T(8,128)(2,1)S(1)} fusion(f32[320,2048]{1,0:T(8,128)S(1)} %fusion.6, bf16[1,384,2048]{2,1,0:T(8,128)(2,1)} %collective-permute-done, bf16[320,768]{1,0:T(8,128)(2,1)S(1)} %fusion.11, s32[]{:T(128)S(6)} %select_n.81), kind=kOutput, calls=%fused_computation.8 | convolution fusion | flops 504627200 | bytes 5750788 | tf_op jit(solution)/shard_map/erf,efd->erd/dot_general | solution.py:64
  141.8 1.3 reshape_transpose_reshape.4
  143.1 5.8 %all-to-all-start.1 = ((bf16[16,20,2048]{2,1,0:T(8,128)(2,1)}), bf16[16,20,2048]{2,1,0:T(8,128)(2,1)S(1)}, u32[]{:S(2)}, u32[]{:S(2)}) async-start(bf16[16,20,2048]{2,1,0:T(8,128)(2,1)} %reshape_transpose_reshape.4), calls=%async_computation.1 | async-start | bytes 3145728 | tf_op jit(solution)/shard_map/all_to_all | solution.py:74
  149.2 0.6 multiply_reduce_fusion.1
  149.8 56.2 %psum.7 = f32[]{:T(128)} all-reduce(f32[]{:T(128)} %multiply_reduce_fusion.1), channel_id=1, replica_groups=mesh['dp'=2,'expert'=16] {'dp','expert'}, use_global_device_ids=true, to_apply=%region_11.12 | all-reduce | flops 1 | bytes 8 | tf_op jit(solution)/shard_map/psum | solution.py:80
  206.5 2.0 gather_fusion.2
  209.6 0.3 reshape.179
  209.9 2.3 %gather_fusion.1 = bf16[256,2048]{1,0:T(8,128)(2,1)} fusion(bf16[320,2048]{1,0:T(8,128)(2,1)S(1)} %reshape.179, s32[1024]{0:T(1024)S(1)} %pad_clamp_fusion), kind=kCustom, calls=%fused_computation.1 | custom fusion | bytes 2098176 | tf_op jit(solution)/shard_map/gather | solution.py:76
  212.2 2.4 %reshape.180 = f32[128,2,2048]{2,1,0:T(2,128)S(1)} reshape(bf16[256,2048]{1,0:T(8,128)(2,1)} %gather_fusion.1) | data formatting | bytes 3145728 | tf_op jit(solution)/shard_map/convert_element_type | solution.py:77
  214.6 3.9 %multiply_reduce_fusion = bf16[128,2048]{1,0:T(8,128)(2,1)} fusion(f32[128,2,2048]{2,1,0:T(2,128)S(1)} %reshape.180, f32[128,2]{1,0:T(8,128)S(1)} %copy.29), kind=kLoop, calls=%fused_computation.9 | loop fusion | flops 786432 | bytes 2622464 | tf_op jit(solution)/shard_map/reduce_sum | solution.py:77
  (44 shorter events, 2.7 us)
Async XLA Ops:
  7.2 3.2 %copy-start = (bf16[128,2048]{1,0:T(8,128)(2,1)S(1)}, bf16[128,2048]{1,0:T(8,128)(2,1)}, u32[]{:S(2)}) copy-start(bf16[128,2048]{1,0:T(8,128)(2,1)} %param.6) | copy-start | bytes 1572868
  7.2 1.5 copy-start.3
  7.2 81.7 %all-gather.3.cloned.1.call-start = ((), (), s32[]{:S(2)}) async-start(), calls=%async_computation.2 | async-start | bytes 4718592 | tf_op jit(solution)/shard_map/all_gather | solution.py:56
  7.9 127.3 %all-gather.5.cloned.1.call-start = ((), (), s32[]{:S(2)}) async-start(), calls=%async_computation.3 | async-start | bytes 4718592 | tf_op jit(solution)/shard_map/all_gather | solution.py:56
  14.6 39.3 %all-to-all-start = ((bf16[16,20,2048]{2,1,0:T(8,128)(2,1)}), bf16[16,20,2048]{2,1,0:T(8,128)(2,1)S(1)}, u32[]{:S(2)}, u32[]{:S(2)}) async-start(bf16[16,20,2048]{2,1,0:T(8,128)(2,1)} %broadcast_select_fusion), calls=%async_computation | async-start | bytes 3145728 | tf_op jit(solution)/shard_map/all_to_all | solution.py:51
  22.1 117.4 %collective-permute-start = (bf16[1,384,2048]{2,1,0:T(8,128)(2,1)}, bf16[1,384,2048]{2,1,0:T(8,128)(2,1)}, u32[]{:S(2)}, u32[]{:S(2)}) collective-permute-start(bf16[1,384,2048]{2,1,0:T(8,128)(2,1)} %param.11), channel_id=1, source_target_pairs={{0,16},{16,0},{1,17},{17,1},{2,18},{18,2},{3,19},{19,3},{4,20},{20... | collective-permute-start | bytes 4718600 | tf_op jit(solution)/shard_map/ppermute | solution.py:15
  93.1 45.5 %copy-start.1 = (bf16[1,384,2048]{2,1,0:T(8,128)(2,1)S(1)}, bf16[1,384,2048]{2,1,0:T(8,128)(2,1)}, u32[]{:S(2)}) copy-start(bf16[1,384,2048]{2,1,0:T(8,128)(2,1)} %param.11) | copy-start | bytes 4718596
  143.1 5.8 %copy-start.2 = (bf16[2048,16]{0,1:T(8,128)(2,1)S(1)}, bf16[2048,16]{0,1:T(8,128)(2,1)}, u32[]{:S(2)}) copy-start(bf16[2048,16]{0,1:T(8,128)(2,1)} %param.7) | copy-start | bytes 196612
  143.1 66.5 %all-to-all-start.1 = ((bf16[16,20,2048]{2,1,0:T(8,128)(2,1)}), bf16[16,20,2048]{2,1,0:T(8,128)(2,1)S(1)}, u32[]{:S(2)}, u32[]{:S(2)}) async-start(bf16[16,20,2048]{2,1,0:T(8,128)(2,1)} %reshape_transpose_reshape.4), calls=%async_computation.1 | async-start | bytes 3145728 | tf_op jit(solution)/shard_map/all_to_all | solution.py:74
Sparse Core Ops, SparseCore 0:
  9.5 79.3 all-gather.2
  90.5 44.7 all-gather.4
